TPU v7x, 256 devices: a whole 4x4x8 slice. The times are simulated.
256 devices in a mesh: grp: 4 (over y), col: 64 (over x, z, core).
Axes of the slice: x: 4, y: 4, z: 8, core: 2. Of those that a mesh axis runs over, the one named last changes fastest.
Arguments:
- panels: bfloat16 [256, 4, 512, 512], P('col', None, 'grp'), may hold values from -1.296875 to 1.296875
- parent: float32 [256, 512, 512], P('col', 'grp'), may hold values from -6 to 6
- src_block: int32 [64, 40], P('col'), may hold values from 0 to 39, each once within a row
- dest_owner: int32 [2560, 1], P('col'), may hold values from 0 to 63; in each aligned block of 40 rows (0 to 39, 40 to 79, ...) no two rows name the same one
- target: int32 [2560], P('col'), may hold values from 0 to 3
- counts: int32 [64], P('col'), may hold values from 20 to 40, as said below
Outputs:
- assembled: float32 [256, 512, 512], P('col', 'grp')
Inputs may be any that keep to these rules, and one draw needn't show every extreme that they name: `src_block`: each row of a column rank is a permutation of the 40 block pairs. `dest_owner`: among the 40 slots of one column rank at most 1 name the same owner. The live slots of a rank are its first counts[c]; some rank has all 40 live.
All inputs are finite; a program needn't handle non-finite values.
Results may differ from a plain program's by a relative error of at most 0.0026.
Values may be sent and summed in bfloat16 or wider, within the bound.
A program may use at most 128 MiB of HBM per device.

v0:
```python
import jax
import jax.numpy as jnp
import numpy as np
from jax import lax
from jax.sharding import PartitionSpec as P


def place_slots(src_block, dest_owner, target, counts, peer_count, capacity):
    slot_count = src_block.shape[1]
    slot_index = jnp.arange(slot_count, dtype=jnp.int32)
    owner_rank = dest_owner[:, 0]
    matches = (owner_rank[:, None] == jnp.arange(peer_count, dtype=jnp.int32)[None, :]).astype(
        jnp.int32
    )
    earlier = jnp.cumsum(matches, axis=0) - matches
    rank_in = jnp.sum(earlier * matches, axis=1)
    position = owner_rank * capacity + rank_in
    is_live = slot_index < counts[0]
    routed = jnp.zeros((peer_count * capacity,), jnp.int32).at[position].set(target)
    return (src_block[0], position, is_live, routed.reshape(peer_count, capacity))


def pack_updates(flat_updates, chosen, position, is_live, peer_count, capacity):
    picked = flat_updates[chosen]
    picked = jnp.where(is_live[:, None, None], picked, jnp.zeros_like(picked))
    buffer = (
        jnp.zeros((peer_count * capacity,) + picked.shape[1:], picked.dtype)
        .at[position]
        .set(picked)
    )
    return buffer.reshape((peer_count, capacity) + picked.shape[1:])


def assemble(received, labels, targets):
    arrived = received.reshape((-1,) + received.shape[2:])
    flat_labels = labels.reshape(-1)
    select = (flat_labels[None, :] == jnp.arange(targets, dtype=jnp.int32)[:, None]).astype(
        jnp.bfloat16
    )
    return jnp.einsum("tn,nrc->trc", select, arrived, preferred_element_type=jnp.float32)


def pair_products(own_rows, piece_rows):
    blocks = own_rows.shape[1]
    upper_table = np.array([a for a in range(blocks) for b in range(a + 1)], np.int32)
    lower_table = np.array([b for a in range(blocks) for b in range(a + 1)], np.int32)
    left_rows = own_rows[:, upper_table]
    right_rows = piece_rows[:, lower_table]
    return jnp.einsum(
        "fprw,fpcw->fprc", left_rows, right_rows, preferred_element_type=jnp.float32
    ).astype(jnp.bfloat16)


def per_device(panels, parent, src_block, dest_owner, target, counts):
    fronts, blocks, quarter, _ = panels.shape
    pair_count = blocks * (blocks + 1) // 2
    peer_count = lax.axis_size("col")
    slot_count = src_block.shape[1]
    capacity = (slot_count + peer_count - 1) // peer_count + slot_count // (2 * peer_count)
    targets = parent.shape[0]
    chosen, position, is_live, routed = place_slots(
        src_block, dest_owner, target, counts, peer_count, capacity
    )
    products = pair_products(panels, lax.all_gather(panels, "grp", axis=2, tiled=True))
    flat_updates = products.reshape(fronts * pair_count, quarter, products.shape[3])
    buffer = pack_updates(flat_updates, chosen, position, is_live, peer_count, capacity)
    received, labels = (
        lax.all_to_all(buffer, "col", split_axis=0, concat_axis=0, tiled=True),
        lax.all_to_all(routed, "col", split_axis=0, concat_axis=0, tiled=True),
    )
    return parent - assemble(received, labels, targets)


def solution(mesh):
    placed = (
        P("col", None, "grp", None),
        P("col", "grp", None),
        P("col", None),
        P("col", None),
        P("col"),
        P("col"),
    )
    return jax.shard_map(
        per_device, mesh=mesh, in_specs=placed, out_specs=P("col", "grp", None), check_vma=False
    )
```

profile of v0, /device:TPU:1, one launch (start us, length us, event | category | flops | bytes accessed | tf_op | source)
XLA Modules:
  0.0 390.6 jit_solution(11302547754613624316)
XLA Ops:
  6.5 0.7 all-gather.2.cloned.1.call-update
  7.3 0.7 fusion.13
  8.1 0.8 select_reduce_fusion
  8.9 0.7 fusion.17
  9.6 0.8 scatter_custom_fusion
  10.4 0.7 copy.36
  11.1 13.0 %all-to-all-start = ((s32[64,1,1]{2,1,0:T(1,128)}), s32[64,1,1]{2,1,0:T(1,128)S(1)}, u32[]{:S(2)}, u32[]{:S(2)}) async-start(s32[64,1,1]{2,1,0:T(1,128)} %copy.36), calls=%async_computation | async-start | bytes 65536 | tf_op jit(solution)/shard_map/all_to_all | solution.py:69
  24.1 0.7 pad_clamp_fusion.2
  24.8 5.7 %gather_fusion = bf16[10,4,128,512]{3,2,1,0:T(8,128)(2,1)} fusion(bf16[4,4,128,512]{3,2,1,0:T(8,128)(2,1)} %param.10, s32[1024]{0:T(1024)S(1)} %pad_clamp_fusion.2), kind=kCustom, calls=%fused_computation | custom fusion | bytes 10485800 | tf_op jit(solution)/shard_map/gather | solution.py:47
  31.2 67.3 %all-gather.2.cloned.1.call-done = bf16[4,4,512,512]{3,2,1,0:T(8,128)(2,1)} async-done(((bf16[4,4,128,512]{3,2,1,0:T(8,128)(2,1)}), bf16[4,4,512,512]{3,2,1,0:T(8,128)(2,1)}) %all-gather.2.cloned.1.call-update) | async-done | bytes 8388624 | tf_op jit(solution)/shard_map/all_gather | solution.py:64
  98.4 6.0 %fusion.22 = (bf16[4,4,256,512]{3,2,1,0:T(8,128)(2,1)}, bf16[4,4,256,512]{3,2,1,0:T(8,128)(2,1)}) fusion(bf16[4,4,512,512]{3,2,1,0:T(8,128)(2,1)} %all-gather.2.cloned.1.call-done), kind=kLoop, calls=%fused_computation.37 | loop fusion | bytes 16777216 | tf_op jit(solution)/shard_map/gather | solution.py:48
  104.5 7.6 %gather_fusion.2 = bf16[10,4,256,512]{3,2,1,0:T(8,128)(2,1)} fusion(bf16[4,4,256,512]{3,2,1,0:T(8,128)(2,1)} %get-tuple-element.5, s32[1024]{0:T(1024)S(1)} %pad_clamp_fusion.1), kind=kCustom, calls=%fused_computation.2 | custom fusion | bytes 20971560 | tf_op jit(solution)/shard_map/gather | solution.py:48
  112.1 7.7 %gather_fusion.3 = bf16[10,4,256,512]{3,2,1,0:T(8,128)(2,1)} fusion(bf16[4,4,256,512]{3,2,1,0:T(8,128)(2,1)} %get-tuple-element.6, s32[1024]{0:T(1024)S(1)} %pad_clamp_fusion.1), kind=kCustom, calls=%fused_computation.3 | custom fusion | bytes 20971560 | tf_op jit(solution)/shard_map/gather | solution.py:48
  119.7 12.3 %copy_bitcast_fusion = (bf16[4,10,256,512]{3,2,1,0:T(8,128)(2,1)S(1)}, bf16[4,10,256,512]{3,2,1,0:T(8,128)(2,1)}) fusion(bf16[10,4,256,512]{3,2,1,0:T(8,128)(2,1)} %gather_fusion.3, bf16[10,4,256,512]{3,2,1,0:T(8,128)(2,1)} %gather_fusion.2), kind=kLoop, calls=%fused_computation.10 | loop fusion | bytes 41943040 | tf_op jit(solution)/shard_map/gather | solution.py:48
  132.1 10.5 %fusion.8 = bf16[4,10,128,512]{3,2,1,0:T(8,128)(2,1)} fusion(bf16[4,10,256,512]{3,2,1,0:T(8,128)(2,1)S(1)} %get-tuple-element.7, bf16[4,10,256,512]{3,2,1,0:T(8,128)(2,1)} %get-tuple-element.8, bf16[10,4,128,512]{3,2,1,0:T(8,128)(2,1)S(1)} %bitcast.34), kind=kOutput, calls=%fused_computation.17 | convolution fusion | flops 2728919040 | bytes 31457280 | tf_op jit(solution)/shard_map/fprw,fpcw->fprc/dot_general | solution.py:49
  142.6 7.2 %gather_fusion.1 = bf16[40,128,512]{2,1,0:T(8,128)(2,1)} fusion(bf16[40,128,512]{2,1,0:T(8,128)(2,1)} %bitcast.35, s32[1024]{0:T(1024)S(1)} %pad_clamp_fusion), kind=kCustom, calls=%fused_computation.1 | custom fusion | bytes 10485920 | tf_op jit(solution)/shard_map/gather | solution.py:24
  149.8 5.3 %broadcast_select_fusion = bf16[40,128,512]{2,1,0:T(8,128)(2,1)} fusion(bf16[40,128,512]{2,1,0:T(8,128)(2,1)} %gather_fusion.1, pred[40]{0:T(512)(128)(4,1)S(1)} %iota_compare_fusion.2), kind=kLoop, calls=%fused_computation.16 | loop fusion | flops 2621440 | bytes 10485800 | tf_op jit(solution)/shard_map/jit(_where)/select_n | solution.py:25
  155.1 4.2 %broadcast_in_dim.30 = bf16[64,128,512]{2,1,0:T(8,128)(2,1)} broadcast(bf16[]{:T(256)} %constant.10.clone.1), dimensions={} | broadcast | bytes 8388610 | tf_op jit(solution)/shard_map/broadcast_in_dim | solution.py:27
  159.3 14.1 %scatter_fusion = bf16[64,128,512]{2,1,0:T(8,128)(2,1)} fusion(bf16[64,128,512]{2,1,0:T(8,128)(2,1)} %broadcast_in_dim.30, s32[40]{0:T(128)S(1)} %fusion.17, bf16[40,128,512]{2,1,0:T(8,128)(2,1)} %broadcast_select_fusion), kind=kCustom, calls=%fused_computation.5 | custom fusion | bytes 15728800 | tf_op jit(solution)/shard_map/scatter | solution.py:29
  173.4 11.0 %all-to-all-start.1 = ((bf16[64,1,128,512]{3,2,1,0:T(8,128)(2,1)}), bf16[64,1,128,512]{3,2,1,0:T(8,128)(2,1)}, u32[]{:S(2)}, u32[]{:S(2)}) async-start(bf16[64,1,128,512]{3,2,1,0:T(8,128)(2,1)} %bitcast.32), calls=%async_computation.1 | async-start | bytes 16777216 | tf_op jit(solution)/shard_map/all_to_all | solution.py:68
  184.4 1.2 reduce
  185.6 184.5 %all-to-all-done.1 = bf16[64,1,128,512]{3,2,1,0:T(8,128)(2,1)} async-done(((bf16[64,1,128,512]{3,2,1,0:T(8,128)(2,1)}), bf16[64,1,128,512]{3,2,1,0:T(8,128)(2,1)}, u32[]{:S(2)}, u32[]{:S(2)}) %all-to-all-start.1) | async-done | bytes 8388640 | tf_op jit(solution)/shard_map/all_to_all | solution.py:68
  370.1 12.3 %fusion.4 = f32[4,128,512]{2,0,1:T(4,128)S(1)} fusion(bf16[64,1,128,512]{3,2,1,0:T(8,128)(2,1)} %all-to-all-done.1, s32[64]{0:T(128)S(1)} %reduce), kind=kOutput, calls=%fused_computation.12 | convolution fusion | flops 33554688 | bytes 9437440 | tf_op jit(solution)/shard_map/tn,nrc->trc/dot_general | solution.py:40
  382.3 1.4 copy_subtract_fusion
  (18 shorter events, 0.1 us)
Async XLA Ops:
  6.5 24.6 %copy-start.1 = (s32[10]{0:T(128)S(1)}, s32[10]{0:T(128)}, u32[]{:S(2)}) copy-start(s32[10]{0:T(128)} %constant.35) | copy-start | bytes 124
  6.5 24.6 %copy-start.2 = (s32[1,40]{1,0:T(1,128)S(1)}, s32[1,40]{1,0:T(1,128)}, u32[]{:S(2)}) copy-start(s32[1,40]{1,0:T(1,128)} %param.12) | copy-start | bytes 484
  6.5 91.9 %all-gather.2.cloned.1.call-start = ((), (), s32[]{:S(2)}) async-start(), calls=%async_computation.2 | async-start | bytes 10485760 | tf_op jit(solution)/shard_map/all_gather | solution.py:64
  11.1 162.3 %all-to-all-start = ((s32[64,1,1]{2,1,0:T(1,128)}), s32[64,1,1]{2,1,0:T(1,128)S(1)}, u32[]{:S(2)}, u32[]{:S(2)}) async-start(s32[64,1,1]{2,1,0:T(1,128)} %copy.36), calls=%async_computation | async-start | bytes 65536 | tf_op jit(solution)/shard_map/all_to_all | solution.py:69
  112.1 20.0 %slice-start = ((s8[5242880]{0:T(1024)(128)(4,1)}), s8[1048576]{0:T(1024)(128)(4,1)S(1)}, s32[]{:S(2)}) async-start(s8[5242880]{0:T(1024)(128)(4,1)} %bitcast.33), calls=%async_computation.3 | async-start | bytes 2097152
  119.7 12.4 %slice-start.1 = ((s8[5242880]{0:T(1024)(128)(4,1)}), s8[4194304]{0:T(1024)(128)(4,1)S(1)}, s32[]{:S(2)}) async-start(s8[5242880]{0:T(1024)(128)(4,1)} %bitcast.33), calls=%async_computation.4 | async-start | bytes 8388608
  173.4 196.7 %all-to-all-start.1 = ((bf16[64,1,128,512]{3,2,1,0:T(8,128)(2,1)}), bf16[64,1,128,512]{3,2,1,0:T(8,128)(2,1)}, u32[]{:S(2)}, u32[]{:S(2)}) async-start(bf16[64,1,128,512]{3,2,1,0:T(8,128)(2,1)} %bitcast.32), calls=%async_computation.1 | async-start | bytes 16777216 | tf_op jit(solution)/shard_map/all_to_all | solution.py:68
  184.3 198.0 %copy-start = (f32[4,128,512]{2,1,0:T(8,128)S(1)}, f32[4,128,512]{2,1,0:T(8,128)}, u32[]{:S(2)}) copy-start(f32[4,128,512]{2,1,0:T(8,128)} %param.11) | copy-start | bytes 3145732
Sparse Core Ops, SparseCore 0:
  9.1 89.2 all-gather.1
where the time goes:
time: 391 us
  waiting for transfers between devices  252 us (64%)
  local copies, waits for them, and re-layouts  66.4 us (17%)
  starting transfers between devices  23.9 us (6%)
  matrix products  22.8 us (6%)
  between operations  14.1 us (4%)
  other arithmetic  10.9 us (3%)
    all_to_all x1, waiting for transfers between devices, per_device(): lax.all_to_all(buffer, 'col', split_axis=0, concat_axis=0, tiled=True)  184 us
    all_gather x1, waiting for transfers between devices, per_device(): lax.all_gather(panels, 'grp', axis=2, tiled=True)  67.3 us
    gather x4, local copies, waits for them, and re-layouts, pair_products(): right_rows = piece_rows[:, lower_table]  33.6 us
    scatter x1, local copies, waits for them, and re-layouts, pack_updates(): buffer = jnp.zeros((peer_count * capacity,) + picked.shape[1:], picked.dt...  14.1 us
    all_to_all x1, starting transfers between devices, per_device(): lax.all_to_all(routed, 'col', split_axis=0, concat_axis=0, tiled=True)  13 us
    dot_general x1, matrix products, assemble(): jnp.einsum('tn,nrc->trc', select, arrived, preferred_element_type=jnp.flo...  12.3 us
    all_to_all x1, starting transfers between devices, per_device(): lax.all_to_all(buffer, 'col', split_axis=0, concat_axis=0, tiled=True)  11 us
    dot_general x1, matrix products, pair_products(): jnp.einsum('fprw,fpcw->fprc', left_rows, right_rows, preferred_element_ty...  10.5 us
  transfers between devices with their start and end apart: 3, of which 2 were waited for; matrix products, arithmetic and copies ran while one was open for 22% of the time, Pallas kernels for 0%

commit v1 on v0

--- a/solution.py
+++ b/solution.py
@@ -61,7 +61,12 @@
     chosen, position, is_live, routed = place_slots(
         src_block, dest_owner, target, counts, peer_count, capacity
     )
-    products = pair_products(panels, lax.all_gather(panels, "grp", axis=2, tiled=True))
+    products = pair_products(
+        panels,
+        jnp.concatenate(
+            lax.all_to_all(jnp.stack([panels] * lax.axis_size("grp")), "grp", 0, 0), axis=2
+        ),
+    )
     flat_updates = products.reshape(fronts * pair_count, quarter, products.shape[3])
     buffer = pack_updates(flat_updates, chosen, position, is_live, peer_count, capacity)
     received, labels = (

time: 391 us -> 412 us (1.054)
  waiting for transfers between devices: 252 us -> 270 us
  between operations: 14.1 us -> 0.8 us
  local copies, waits for them, and re-layouts: 66.4 us -> 77.9 us
  starting transfers between devices: 23.9 us -> 31 us
    all_to_all x0 -> x1, waiting for transfers between devices: none -> 85.8 us  [per_device(): lax.all_to_all(jnp.stack([panels] * lax.axis_size('grp')), 'grp', 0, 0)]
    all_gather x1 -> x0, waiting for transfers between devices: 67.3 us -> none  [per_device(): lax.all_gather(panels, 'grp', axis=2, tiled=True)]
    all_to_all x0 -> x1, local copies, waits for them, and re-layouts: none -> 7.59 us  [per_device(): lax.all_to_all(jnp.stack([panels] * lax.axis_size('grp')), 'grp', 0, 0)]
    another operation x0 -> x1, local copies, waits for them, and re-layouts: none -> 5.98 us  [per_device(): jnp.stack([panels] * lax.axis_size('grp'))]
    all_to_all x0 -> x1, starting transfers between devices: none -> 5.77 us  [per_device(): lax.all_to_all(jnp.stack([panels] * lax.axis_size('grp')), 'grp', 0, 0)]
where the time goes in v1:
time: 412 us; the launch traced here: 411 us
  waiting for transfers between devices  270 us (66%)
  local copies, waits for them, and re-layouts  77.9 us (19%)
  starting transfers between devices  31 us (8%)
  matrix products  22.8 us (6%)
  other arithmetic  8.25 us (2%)
    all_to_all x1, waiting for transfers between devices, per_device(): lax.all_to_all(buffer, 'col', split_axis=0, concat_axis=0, tiled=True)  184 us
    all_to_all x1, waiting for transfers between devices, per_device(): lax.all_to_all(jnp.stack([panels] * lax.axis_size('grp')), 'grp', 0, 0)  85.8 us
    gather x4, local copies, waits for them, and re-layouts, pair_products(): right_rows = piece_rows[:, lower_table]  33.5 us
    all_to_all x1, starting transfers between devices, per_device(): lax.all_to_all(routed, 'col', split_axis=0, concat_axis=0, tiled=True)  14.9 us
    scatter x1, local copies, waits for them, and re-layouts, pack_updates(): buffer = jnp.zeros((peer_count * capacity,) + picked.shape[1:], picked.dt...  14.1 us
    dot_general x1, matrix products, assemble(): jnp.einsum('tn,nrc->trc', select, arrived, preferred_element_type=jnp.flo...  12.3 us
    dot_general x1, matrix products, pair_products(): jnp.einsum('fprw,fpcw->fprc', left_rows, right_rows, preferred_element_ty...  10.5 us
    all_to_all x1, starting transfers between devices, per_device(): lax.all_to_all(buffer, 'col', split_axis=0, concat_axis=0, tiled=True)  10.4 us
  transfers between devices with their start and end apart: 3, of which 2 were waited for; matrix products, arithmetic and copies ran while one was open for 22% of the time, Pallas kernels for 0%

profile of v1, /device:TPU:1, one launch (start us, length us, event | category | flops | bytes accessed | tf_op | source)
XLA Modules:
  0.0 411.0 jit_solution(55861167895573299)
XLA Ops:
  0.0 6.0 %stack.2 = bf16[4,4,4,128,512]{4,3,2,1,0:T(8,128)(2,1)} broadcast(bf16[4,4,128,512]{3,2,1,0:T(8,128)(2,1)} %param.10), dimensions={1,2,3,4} | broadcast | bytes 10485760 | tf_op jit(solution)/shard_map/stack | solution.py:67
  6.0 5.8 %all-to-all-start.1 = ((bf16[4,4,4,128,512]{4,3,2,1,0:T(8,128)(2,1)}), bf16[4,4,4,128,512]{4,3,2,1,0:T(8,128)(2,1)}, u32[]{:S(2)}, u32[]{:S(2)}) async-start(bf16[4,4,4,128,512]{4,3,2,1,0:T(8,128)(2,1)} %stack.2), calls=%async_computation.1 | async-start | bytes 16777216 | tf_op jit(solution)/shard_map/all_to_all | solution.py:67
  11.8 3.8 gather_fusion
  16.3 0.1 fusion.13
  16.4 0.2 select_reduce_fusion
  16.6 0.8 scatter_custom_fusion
  17.4 0.7 copy.38
  18.2 85.8 %all-to-all-done.1 = bf16[4,4,4,128,512]{4,3,2,1,0:T(8,128)(2,1)} async-done(((bf16[4,4,4,128,512]{4,3,2,1,0:T(8,128)(2,1)}), bf16[4,4,4,128,512]{4,3,2,1,0:T(8,128)(2,1)}, u32[]{:S(2)}, u32[]{:S(2)}) %all-to-all-start.1) | async-done | bytes 8388640 | tf_op jit(solution)/shard_map/all_to_all | solution.py:67
  104.0 14.9 %all-to-all-start = ((s32[64,1,1]{2,1,0:T(1,128)}), s32[64,1,1]{2,1,0:T(1,128)S(1)}, u32[]{:S(2)}, u32[]{:S(2)}) async-start(s32[64,1,1]{2,1,0:T(1,128)} %copy.38), calls=%async_computation | async-start | bytes 65536 | tf_op jit(solution)/shard_map/all_to_all | solution.py:74
  118.8 7.6 %copy.39 = bf16[4,4,4,128,512]{4,3,0,2,1:T(8,128)(2,1)} copy(bf16[4,4,4,128,512]{4,3,2,1,0:T(8,128)(2,1)} %all-to-all-done.1) | data formatting | bytes 16777216 | tf_op jit(solution)/shard_map/all_to_all | solution.py:67
  126.4 5.8 %fusion.22 = (bf16[4,4,256,512]{3,2,1,0:T(8,128)(2,1)}, bf16[4,4,256,512]{3,2,1,0:T(8,128)(2,1)}) fusion(bf16[4,4,512,512]{3,2,1,0:T(8,128)(2,1)} %bitcast.36), kind=kLoop, calls=%fused_computation.37 | loop fusion | bytes 16777216 | tf_op jit(solution)/shard_map/gather | solution.py:48
  132.2 7.6 %gather_fusion.2 = bf16[10,4,256,512]{3,2,1,0:T(8,128)(2,1)} fusion(bf16[4,4,256,512]{3,2,1,0:T(8,128)(2,1)} %get-tuple-element.5, s32[1024]{0:T(1024)S(1)} %pad_clamp_fusion.1), kind=kCustom, calls=%fused_computation.2 | custom fusion | bytes 20971560 | tf_op jit(solution)/shard_map/gather | solution.py:48
  139.8 7.7 %gather_fusion.3 = bf16[10,4,256,512]{3,2,1,0:T(8,128)(2,1)} fusion(bf16[4,4,256,512]{3,2,1,0:T(8,128)(2,1)} %get-tuple-element.6, s32[1024]{0:T(1024)S(1)} %pad_clamp_fusion.1), kind=kCustom, calls=%fused_computation.3 | custom fusion | bytes 20971560 | tf_op jit(solution)/shard_map/gather | solution.py:48
  147.5 12.4 %copy_bitcast_fusion = (bf16[4,10,256,512]{3,2,1,0:T(8,128)(2,1)S(1)}, bf16[4,10,256,512]{3,2,1,0:T(8,128)(2,1)}) fusion(bf16[10,4,256,512]{3,2,1,0:T(8,128)(2,1)} %gather_fusion.3, bf16[10,4,256,512]{3,2,1,0:T(8,128)(2,1)} %gather_fusion.2), kind=kLoop, calls=%fused_computation.10 | loop fusion | bytes 41943040 | tf_op jit(solution)/shard_map/gather | solution.py:48
  159.9 10.5 %fusion.8 = bf16[4,10,128,512]{3,2,1,0:T(8,128)(2,1)} fusion(bf16[4,10,256,512]{3,2,1,0:T(8,128)(2,1)S(1)} %get-tuple-element.7, bf16[4,10,256,512]{3,2,1,0:T(8,128)(2,1)} %get-tuple-element.8, bf16[10,4,128,512]{3,2,1,0:T(8,128)(2,1)S(1)} %bitcast.38), kind=kOutput, calls=%fused_computation.17 | convolution fusion | flops 2728919040 | bytes 31457280 | tf_op jit(solution)/shard_map/fprw,fpcw->fprc/dot_general | solution.py:49
  170.4 7.2 %gather_fusion.1 = bf16[40,128,512]{2,1,0:T(8,128)(2,1)} fusion(bf16[40,128,512]{2,1,0:T(8,128)(2,1)} %bitcast.39, s32[1024]{0:T(1024)S(1)} %pad_clamp_fusion), kind=kCustom, calls=%fused_computation.1 | custom fusion | bytes 10485920 | tf_op jit(solution)/shard_map/gather | solution.py:24
  177.6 5.3 %broadcast_select_fusion = bf16[40,128,512]{2,1,0:T(8,128)(2,1)} fusion(bf16[40,128,512]{2,1,0:T(8,128)(2,1)} %gather_fusion.1, pred[40]{0:T(512)(128)(4,1)S(1)} %iota_compare_fusion.2), kind=kLoop, calls=%fused_computation.16 | loop fusion | flops 2621440 | bytes 10485800 | tf_op jit(solution)/shard_map/jit(_where)/select_n | solution.py:25
  182.8 4.2 %broadcast_in_dim.30 = bf16[64,128,512]{2,1,0:T(8,128)(2,1)} broadcast(bf16[]{:T(256)} %constant.10.clone.1), dimensions={} | broadcast | bytes 8388610 | tf_op jit(solution)/shard_map/broadcast_in_dim | solution.py:27
  187.1 14.1 %scatter_fusion = bf16[64,128,512]{2,1,0:T(8,128)(2,1)} fusion(bf16[64,128,512]{2,1,0:T(8,128)(2,1)} %broadcast_in_dim.30, s32[40]{0:T(128)S(1)} %fusion.17, bf16[40,128,512]{2,1,0:T(8,128)(2,1)} %broadcast_select_fusion), kind=kCustom, calls=%fused_computation.5 | custom fusion | bytes 15728800 | tf_op jit(solution)/shard_map/scatter | solution.py:29
  201.2 10.4 %all-to-all-start.2 = ((bf16[64,1,128,512]{3,2,1,0:T(8,128)(2,1)}), bf16[64,1,128,512]{3,2,1,0:T(8,128)(2,1)}, u32[]{:S(2)}, u32[]{:S(2)}) async-start(bf16[64,1,128,512]{3,2,1,0:T(8,128)(2,1)} %bitcast.35), calls=%async_computation.2 | async-start | bytes 16777216 | tf_op jit(solution)/shard_map/all_to_all | solution.py:73
  211.6 1.2 reduce
  212.8 184.5 %all-to-all-done.2 = bf16[64,1,128,512]{3,2,1,0:T(8,128)(2,1)} async-done(((bf16[64,1,128,512]{3,2,1,0:T(8,128)(2,1)}), bf16[64,1,128,512]{3,2,1,0:T(8,128)(2,1)}, u32[]{:S(2)}, u32[]{:S(2)}) %all-to-all-start.2) | async-done | bytes 8388640 | tf_op jit(solution)/shard_map/all_to_all | solution.py:73
  397.3 12.3 %fusion.4 = f32[4,128,512]{2,0,1:T(4,128)S(1)} fusion(bf16[64,1,128,512]{3,2,1,0:T(8,128)(2,1)} %all-to-all-done.2, s32[64]{0:T(128)S(1)} %reduce), kind=kOutput, calls=%fused_computation.12 | convolution fusion | flops 33554688 | bytes 9437440 | tf_op jit(solution)/shard_map/tn,nrc->trc/dot_general | solution.py:40
  409.6 1.4 copy_subtract_fusion
  (25 shorter events, 0.1 us)
Async XLA Ops:
  6.0 5.8 %copy-start.4 = (s32[10]{0:T(128)S(1)}, s32[10]{0:T(128)}, u32[]{:S(2)}) copy-start(s32[10]{0:T(128)} %constant.34) | copy-start | bytes 124
  6.0 5.8 %copy-start = (bf16[4,4,128,512]{3,2,1,0:T(8,128)(2,1)S(1)}, bf16[4,4,128,512]{3,2,1,0:T(8,128)(2,1)}, u32[]{:S(2)}) copy-start(bf16[4,4,128,512]{3,2,1,0:T(8,128)(2,1)} %param.10) | copy-start | bytes 6291460
  6.0 98.0 %all-to-all-start.1 = ((bf16[4,4,4,128,512]{4,3,2,1,0:T(8,128)(2,1)}), bf16[4,4,4,128,512]{4,3,2,1,0:T(8,128)(2,1)}, u32[]{:S(2)}, u32[]{:S(2)}) async-start(bf16[4,4,4,128,512]{4,3,2,1,0:T(8,128)(2,1)} %stack.2), calls=%async_computation.1 | async-start | bytes 16777216 | tf_op jit(solution)/shard_map/all_to_all | solution.py:67
  11.8 4.5 %copy-start.2 = (s32[40,1]{0,1:T(1,128)S(1)}, s32[40,1]{0,1:T(1,128)}, u32[]{:S(2)}) copy-start(s32[40,1]{0,1:T(1,128)} %param.13) | copy-start | bytes 484
  11.8 6.4 %copy-start.3 = (s32[10]{0:T(128)S(1)}, s32[10]{0:T(128)}, u32[]{:S(2)}) copy-start(s32[10]{0:T(128)} %constant.35) | copy-start | bytes 124
  11.8 6.4 %copy-start.5 = (s32[1,40]{1,0:T(1,128)S(1)}, s32[1,40]{1,0:T(1,128)}, u32[]{:S(2)}) copy-start(s32[1,40]{1,0:T(1,128)} %param.12) | copy-start | bytes 484
  104.0 97.2 %all-to-all-start = ((s32[64,1,1]{2,1,0:T(1,128)}), s32[64,1,1]{2,1,0:T(1,128)S(1)}, u32[]{:S(2)}, u32[]{:S(2)}) async-start(s32[64,1,1]{2,1,0:T(1,128)} %copy.38), calls=%async_computation | async-start | bytes 65536 | tf_op jit(solution)/shard_map/all_to_all | solution.py:74
  139.8 20.0 %slice-start = ((s8[5242880]{0:T(1024)(128)(4,1)}), s8[1048576]{0:T(1024)(128)(4,1)S(1)}, s32[]{:S(2)}) async-start(s8[5242880]{0:T(1024)(128)(4,1)} %bitcast.37), calls=%async_computation.3 | async-start | bytes 2097152
  147.5 12.4 %slice-start.1 = ((s8[5242880]{0:T(1024)(128)(4,1)}), s8[4194304]{0:T(1024)(128)(4,1)S(1)}, s32[]{:S(2)}) async-start(s8[5242880]{0:T(1024)(128)(4,1)} %bitcast.37), calls=%async_computation.4 | async-start | bytes 8388608
  201.2 196.1 %all-to-all-start.2 = ((bf16[64,1,128,512]{3,2,1,0:T(8,128)(2,1)}), bf16[64,1,128,512]{3,2,1,0:T(8,128)(2,1)}, u32[]{:S(2)}, u32[]{:S(2)}) async-start(bf16[64,1,128,512]{3,2,1,0:T(8,128)(2,1)} %bitcast.35), calls=%async_computation.2 | async-start | bytes 16777216 | tf_op jit(solution)/shard_map/all_to_all | solution.py:73
  211.6 198.0 %copy-start.1 = (f32[4,128,512]{2,1,0:T(8,128)S(1)}, f32[4,128,512]{2,1,0:T(8,128)}, u32[]{:S(2)}) copy-start(f32[4,128,512]{2,1,0:T(8,128)} %param.11) | copy-start | bytes 3145732
